TPU v7x, 32 devices: a whole 2x2x4 slice. The times are simulated.
32 devices in a mesh: dp: 8 (over z, x), expert: 4 (over y, core).
Axes of the slice: x: 2, y: 2, z: 4, core: 2. Of those that a mesh axis runs over, the one named last changes fastest.
Arguments:
- tokens: bfloat16 [4096, 2048], P(('dp', 'expert')), may hold values from -6 to 6
- out_grad: bfloat16 [4096, 2048], P(('dp', 'expert')), may hold values from -3 to 3
- z_weight: float32 [4096], P(('dp', 'expert')), may hold values from 0.1 to 1
- router_weight: bfloat16 [2048, 128], replicated, may hold values from -0.125 to 0.125
- expert_ids: int32 [4096, 4], P(('dp', 'expert')), may hold values from 0 to 127, as said below
- gate_up_weight: bfloat16 [4, 2048, 3072], P('expert'), may hold values from -0.125 to 0.125
- down_weight: bfloat16 [4, 1536, 2048], P('expert'), may hold values from -0.15625 to 0.15625
Outputs:
- token_grad: bfloat16 [4096, 2048], P(('dp', 'expert'))
- router_grad: float32 [2048, 128], replicated
- gate_up_grad: bfloat16 [4, 2048, 3072], P('expert', 'dp')
- down_grad: bfloat16 [4, 1536, 2048], P('expert', 'dp')
Inputs may be any that keep to these rules, and one draw needn't show every extreme that they name: `expert_ids`: each row names 4 different experts. Experts 0 to 3 are the ones in flight. The 128 rows of one device name any one expert in flight at most 64 times; in every data group some expert in flight is named exactly 64 times by the rows of each device of the group.
All inputs are finite; a program needn't handle non-finite values.
Results may differ from a plain program's by a relative error of at most 0.019.
Values may be sent and summed in bfloat16 or wider, within the bound.
A program may use at most 192 MiB of HBM per device.

v0:
```python
import jax
import jax.numpy as jnp
from jax import lax
from jax.sharding import PartitionSpec as P


def expert_rows(rows_in, rows_grad, w_gateup, w_down, acc_gateup, acc_down):
    hidden_units = w_down.shape[0]
    pre_act = jnp.dot(rows_in, w_gateup, preferred_element_type=jnp.float32)
    gate_pre = pre_act[:, :hidden_units]
    up_pre = pre_act[:, hidden_units:]
    activated = jax.nn.silu(gate_pre)
    hidden = (activated * up_pre).astype(jnp.bfloat16)
    expert_out = jnp.dot(hidden, w_down, preferred_element_type=jnp.float32).astype(jnp.bfloat16)
    hidden_grad = lax.dot_general(
        rows_grad, w_down, (((1,), (1,)), ((), ())), preferred_element_type=jnp.float32
    )
    acc_down = lax.dot_general(
        hidden, rows_grad, (((0,), (0,)), ((), ())), preferred_element_type=jnp.float32
    )
    sigmoid_gate = jax.nn.sigmoid(gate_pre)
    gate_grad = hidden_grad * up_pre * sigmoid_gate * (1.0 + gate_pre * (1.0 - sigmoid_gate))
    up_grad = hidden_grad * activated
    pre_grad = jnp.concatenate([gate_grad, up_grad], axis=1).astype(jnp.bfloat16)
    acc_gateup = lax.dot_general(
        rows_in, pre_grad, (((0,), (0,)), ((), ())), preferred_element_type=jnp.float32
    )
    input_grad = lax.dot_general(
        pre_grad, w_gateup, (((1,), (1,)), ((), ())), preferred_element_type=jnp.float32
    ).astype(jnp.bfloat16)
    return (acc_gateup, acc_down, expert_out, input_grad)


def split_pair(values):
    upper = values.astype(jnp.bfloat16)
    lower = (values - upper.astype(jnp.float32)).astype(jnp.bfloat16)
    return jnp.stack([upper, lower], axis=-1)


def join_pair(pair):
    return pair[..., 0].astype(jnp.float32) + pair[..., 1].astype(jnp.float32)


def per_device(tokens, out_grad, z_weight, router_weight, expert_ids, gate_up_weight, down_weight):
    tok_count, width = tokens.shape
    top_count = expert_ids.shape[1]
    routed = router_weight.shape[1]
    flight = lax.axis_size("expert")
    capacity = tok_count // 2
    w_gateup = gate_up_weight[0]
    w_down = down_weight[0]
    hidden_units = w_down.shape[0]
    logits = jnp.dot(tokens, router_weight, preferred_element_type=jnp.float32)
    choose = expert_ids[:, :, None] == jnp.arange(routed, dtype=jnp.int32)[None, None, :]
    selected = jnp.sum(jnp.where(choose, logits[:, None, :], 0.0), axis=2)
    sel_exp = jnp.exp(selected)
    probs = sel_exp / jnp.sum(sel_exp, axis=1, keepdims=True)
    log_total = jnp.log(jnp.sum(jnp.exp(logits), axis=1))
    flat_ids = expert_ids.reshape(-1)
    slot_count = tok_count * top_count
    member = (flat_ids[:, None] == jnp.arange(flight, dtype=jnp.int32)[None, :]).astype(jnp.int32)
    ranks = jnp.sum((jnp.cumsum(member, axis=0) - 1) * member, axis=1)
    in_flight = flat_ids < flight
    position = jnp.where(in_flight, flat_ids * capacity + ranks, flight * capacity)
    source_slot = (
        jnp.zeros((flight * capacity,), jnp.int32)
        .at[position]
        .set(jnp.arange(slot_count, dtype=jnp.int32), mode="drop")
    )
    filled = jnp.zeros((flight * capacity,), jnp.bool_).at[position].set(True, mode="drop")
    source_tok = source_slot // top_count
    send_in = jnp.where(filled[:, None], tokens[source_tok], 0)
    slot_prob = jnp.where(filled, probs.reshape(-1)[source_slot], 0.0)
    counts = jnp.sum(member, axis=0)
    count_msg = jnp.stack([counts // 128, counts % 128], axis=1).astype(jnp.bfloat16)
    send_raw = jnp.where(filled[:, None], out_grad[source_tok], 0)
    prob_pair = split_pair(slot_prob)
    recv_in, recv_raw, recv_prob, recv_counts = (
        lax.all_to_all(
            send_in.reshape(flight, capacity, width),
            "expert",
            split_axis=0,
            concat_axis=0,
            tiled=True,
        ),
        lax.all_to_all(
            send_raw.reshape(flight, capacity, width),
            "expert",
            split_axis=0,
            concat_axis=0,
            tiled=True,
        ),
        lax.all_to_all(
            prob_pair.reshape(flight, capacity, 2),
            "expert",
            split_axis=0,
            concat_axis=0,
            tiled=True,
        ),
        lax.all_to_all(count_msg, "expert", split_axis=0, concat_axis=0, tiled=True),
    )
    sources = recv_in.shape[0]
    total_rows = sources * capacity
    flat_in = recv_in.reshape(total_rows, width)
    flat_raw = recv_raw.reshape(total_rows, width)
    row_prob = join_pair(recv_prob.reshape(total_rows, 2))
    flat_grad = (row_prob[:, None] * flat_raw.astype(jnp.float32)).astype(jnp.bfloat16)
    acc_gateup, acc_down, produced, back_rows = expert_rows(
        flat_in,
        flat_grad,
        w_gateup,
        w_down,
        jnp.zeros((width, 2 * hidden_units), jnp.float32),
        jnp.zeros((hidden_units, width), jnp.float32),
    )
    slot_at = jnp.where(in_flight, position, 0)
    row_score = jnp.sum(flat_raw.astype(jnp.float32) * produced.astype(jnp.float32), axis=1)
    score_pair = split_pair(row_score)
    home_dx, home_pair = (
        lax.all_to_all(
            back_rows.reshape(sources, capacity, width),
            "expert",
            split_axis=0,
            concat_axis=0,
            tiled=True,
        ),
        lax.all_to_all(
            score_pair.reshape(sources, capacity, 2),
            "expert",
            split_axis=0,
            concat_axis=0,
            tiled=True,
        ),
    )
    flat_dx = home_dx.reshape(flight * capacity, width)
    flat_score = join_pair(home_pair.reshape(flight * capacity, 2))
    scores = jnp.where(in_flight, flat_score[slot_at], 0.0).reshape(tok_count, top_count)
    slot_dx = jnp.where(in_flight[:, None], flat_dx[slot_at], 0).reshape(
        tok_count, top_count, width
    )
    mean_score = jnp.sum(probs * scores, axis=1, keepdims=True)
    sel_grad = probs * (scores - mean_score)
    z_grad = 2.0 * z_weight[:, None] * log_total[:, None] * jnp.exp(logits - log_total[:, None])
    logit_grad = (z_grad + jnp.sum(jnp.where(choose, sel_grad[:, :, None], 0.0), axis=1)).astype(
        jnp.bfloat16
    )
    token_grad = (
        jnp.sum(slot_dx.astype(jnp.float32), axis=1)
        + lax.dot_general(
            logit_grad, router_weight, (((1,), (1,)), ((), ())), preferred_element_type=jnp.float32
        )
    ).astype(jnp.bfloat16)
    router_part = lax.dot_general(
        tokens, logit_grad, (((0,), (0,)), ((), ())), preferred_element_type=jnp.float32
    )
    router_grad = lax.psum(router_part, ("dp", "expert"))
    part_gateup = acc_gateup.astype(jnp.bfloat16)
    part_down = acc_down.astype(jnp.bfloat16)
    gate_up_grad, down_grad = (
        lax.psum_scatter(part_gateup[None], "dp", scatter_dimension=1, tiled=True).astype(
            jnp.float32
        ),
        lax.psum_scatter(part_down[None], "dp", scatter_dimension=1, tiled=True).astype(
            jnp.float32
        ),
    )
    return (
        token_grad,
        router_grad,
        gate_up_grad.astype(jnp.bfloat16),
        down_grad.astype(jnp.bfloat16),
    )


def solution(mesh):
    return jax.shard_map(
        per_device,
        mesh=mesh,
        in_specs=(
            P(("dp", "expert"), None),
            P(("dp", "expert"), None),
            P(("dp", "expert")),
            P(),
            P(("dp", "expert"), None),
            P("expert", None, None),
            P("expert", None, None),
        ),
        out_specs=(
            P(("dp", "expert"), None),
            P(),
            P("expert", "dp", None),
            P("expert", "dp", None),
        ),
        check_vma=False,
    )
```

profile of v0, /device:TPU:0, one launch (start us, length us, event | category | flops | bytes accessed | tf_op | source)
XLA Modules:
  0.0 440.1 jit_solution(1820209398362379599)
XLA Ops:
  8.0 0.7 broadcast_compare_fusion
  8.8 0.7 broadcast_multiply_fusion
  9.4 0.8 copy.45
  10.6 0.6 copy-done.5
  11.5 1.2 reduce-window.6
  13.3 2.4 scatter_custom_fusion.1
  15.8 2.4 scatter_custom_fusion
  18.3 0.6 pad_clamp_fusion.1
  18.9 1.4 gather_fusion.2
  20.3 1.4 gather_fusion.1
  21.7 1.5 broadcast_select_fusion
  23.2 4.4 all-to-all-start.2
  28.3 0.6 multiply_multiply_fusion
  29.0 13.1 %all-to-all-done.2 = bf16[4,64,2048]{2,1,0:T(8,128)(2,1)S(1)} async-done(((bf16[4,64,2048]{2,1,0:T(8,128)(2,1)}), bf16[4,64,2048]{2,1,0:T(8,128)(2,1)S(1)}, u32[]{:S(2)}, u32[]{:S(2)}) %all-to-all-start.2) | async-done | bytes 1048608 | tf_op jit(solution)/shard_map/all_to_all | solution.py:79
  42.0 3.5 all-to-all-start.1
  45.6 9.7 %fusion.2 = f32[256,3072]{1,0:T(8,128)} fusion(bf16[256,2048]{1,0:T(8,128)(2,1)S(1)} %bitcast.81, bf16[1,2048,3072]{2,1,0:T(8,128)(2,1)} %param.12), kind=kOutput, calls=%fused_computation.9 | convolution fusion | flops 3221225472 | bytes 16777216 | tf_op jit(solution)/shard_map/dot_general | solution.py:9
  55.2 2.3 multiply_convert_fusion.1
  57.6 2.4 all-to-all-done.1
  60.0 4.8 %fusion.24 = f32[256]{0:T(256)S(1)} fusion(bf16[256,1536]{1,0:T(8,128)(2,1)S(1)} %multiply_convert_fusion.1, bf16[1,1536,2048]{2,1,0:T(8,128)(2,1)} %param.13, bf16[256,2048]{1,0:T(8,128)(2,1)S(1)} %bitcast.80), kind=kOutput, calls=%fused_computation.35 | convolution fusion | flops 1613233920 | bytes 8127488 | tf_op jit(solution)/shard_map/dot_general | solution.py:14
  64.8 0.6 copy.51
  65.4 3.4 all-to-all-start.4
  68.8 0.5 exponential_reduce_fusion.1
  69.4 3.0 all-to-all-done.4
  72.4 3.5 gather_fusion.4
  76.1 1.2 multiply_reduce_fusion
  77.3 0.6 copy-done.8
  78.1 2.1 gather_fusion
  80.2 0.6 subtract_convert_fusion.1
  80.8 0.6 select_convert_fusion
  81.4 0.7 subtract_multiply_fusion
  82.2 0.6 copy.49
  82.8 3.2 all-to-all-start
  86.3 0.7 copy.54
  87.0 0.9 add_convert_fusion
  87.9 1.3 convolution_bitcast_fusion
  90.3 0.7 fusion.38
  91.2 4.4 %fusion.4 = bf16[1,1536,2048]{2,1,0:T(8,128)(2,1)} fusion(bf16[256,1536]{1,0:T(8,128)(2,1)S(1)} %multiply_convert_fusion.1, bf16[256,2048]{1,0:T(8,128)(2,1)S(1)} %fusion.22), kind=kOutput, calls=%fused_computation.13 | convolution fusion | flops 1613758464 | bytes 8126464 | tf_op jit(solution)/shard_map/dot_general | solution.py:18
  96.1 6.0 %multiply_convert_fusion.3 = (bf16[256,1536]{1,0:T(8,128)(2,1)S(1)}, bf16[256,1536]{1,0:T(8,128)(2,1)S(1)}) fusion(f32[256,3072]{1,0:T(8,128)} %fusion.2, bf16[256,2048]{1,0:T(8,128)(2,1)S(1)} %bitcast.85, bf16[1,1536,2048]{2,1,0:T(8,128)(2,1)} %param.13), kind=kOutput, calls=%fused_computation.32 | convolution fusion | flops 1615724544 | bytes 12058624 | tf_op jit(solution)/shard_map/dot_general | solution.py:15
  102.1 6.6 %convert_bitcast_fusion = bf16[1,2048,3072]{2,1,0:T(8,128)(2,1)} fusion(bf16[256,2048]{1,0:T(8,128)(2,1)S(1)} %bitcast.82, bf16[256,1536]{1,0:T(8,128)(2,1)S(1)} %get-tuple-element.31, bf16[256,1536]{1,0:T(8,128)(2,1)S(1)} %get-tuple-element.30), kind=kOutput, calls=%fused_computation.11 | convolution fusion | flops 3230662656 | bytes 15204352 | tf_op jit(solution)/shard_map/dot_general | solution.py:25
  108.7 9.0 %fusion.18 = bf16[256,2048]{1,0:T(8,128)(2,1)} fusion(bf16[1,2048,3072]{2,1,0:T(8,128)(2,1)} %param.12, bf16[256,1536]{1,0:T(8,128)(2,1)S(1)} %get-tuple-element.31, bf16[256,1536]{1,0:T(8,128)(2,1)S(1)} %get-tuple-element.30), kind=kOutput, calls=%fused_computation.22 | convolution fusion | flops 3224895488 | bytes 15204352 | tf_op jit(solution)/shard_map/dot_general | solution.py:28
  117.8 3.9 all-to-all-start.3
  121.7 229.6 %all-reduce.2.cloned.1.call-done = f32[2048,128]{0,1:T(8,128)} async-done(((f32[2048,128]{0,1:T(8,128)}), f32[2048,128]{0,1:T(8,128)}) %all-reduce.2.cloned.1.call-update) | async-done | bytes 1048592 | tf_op jit(solution)/shard_map/psum | solution.py:156
  351.2 2.6 copy.55
  353.8 2.5 gather_fusion.3
  356.3 2.2 gather.29
  358.6 5.6 %convert_reduce_fusion = f32[128,2048]{1,0:T(8,128)S(1)} fusion(bf16[128,4,2048]{2,1,0:T(4,128)(2,1)} %gather.29, pred[128,4]{1,0:T(8,128)(4,1)S(1)} %copy-done.6), kind=kLoop, calls=%fused_computation.18 | loop fusion | flops 2883584 | bytes 3146240 | tf_op jit(solution)/shard_map/reduce_sum | solution.py:148
  364.1 1.1 fusion.21
  365.3 67.3 %reduce-scatter.3.cloned.1.call-done = bf16[1,256,3072]{2,1,0:T(8,128)(2,1)} async-done(((bf16[1,2048,3072]{2,1,0:T(8,128)(2,1)}), bf16[1,256,3072]{2,1,0:T(8,128)(2,1)}) %reduce-scatter.3.cloned.1.call-update) | async-done | bytes 1572880 | tf_op jit(solution)/shard_map/reduce_scatter | solution.py:160
  (73 shorter events, 4.8 us)
Async XLA Ops:
  8.0 10.9 %copy-start = (bf16[128,2048]{1,0:T(8,128)(2,1)S(1)}, bf16[128,2048]{1,0:T(8,128)(2,1)}, u32[]{:S(2)}) copy-start(bf16[128,2048]{1,0:T(8,128)(2,1)} %param.7) | copy-start | bytes 1572868
  10.6 0.6 copy-start.5
  18.2 0.7 copy-start.11
  18.9 1.4 copy-start.2
  23.2 4.4 %copy-start.3 = (bf16[2048,128]{1,0:T(8,128)(2,1)S(1)}, bf16[2048,128]{1,0:T(8,128)(2,1)}, u32[]{:S(2)}) copy-start(bf16[2048,128]{1,0:T(8,128)(2,1)} %param.10) | copy-start | bytes 1572868
  23.2 4.9 %copy-start.7 = (s32[128,4]{0,1:T(4,128)S(1)}, s32[128,4]{0,1:T(4,128)}, u32[]{:S(2)}) copy-start(s32[128,4]{0,1:T(4,128)} %param.11) | copy-start | bytes 6148
  23.2 5.1 %copy-start.12 = (f32[128]{0:T(128)S(1)}, f32[128]{0:T(128)}, u32[]{:S(2)}) copy-start(f32[128]{0:T(128)} %param.9) | copy-start | bytes 1540
  23.2 18.8 %all-to-all-start.2 = ((bf16[4,64,2048]{2,1,0:T(8,128)(2,1)}), bf16[4,64,2048]{2,1,0:T(8,128)(2,1)S(1)}, u32[]{:S(2)}, u32[]{:S(2)}) async-start(bf16[4,64,2048]{2,1,0:T(8,128)(2,1)} %get-tuple-element.38), calls=%async_computation.2 | async-start | bytes 2097152 | tf_op jit(solution)/shard_map/all_to_all | solution.py:79
  28.1 44.3 %copy-start.9 = (s32[1024]{0:T(1024)}, s32[1024]{0:T(1024)S(1)}, u32[]{:S(2)}) copy-start(s32[1024]{0:T(1024)S(1)} %pad_clamp_fusion) | copy-start | bytes 12292
  42.0 17.9 %all-to-all-start.1 = ((bf16[4,64,2048]{2,1,0:T(8,128)(2,1)}), bf16[4,64,2048]{2,1,0:T(8,128)(2,1)S(1)}, u32[]{:S(2)}, u32[]{:S(2)}) async-start(bf16[4,64,2048]{2,1,0:T(8,128)(2,1)} %get-tuple-element.39), calls=%async_computation.1 | async-start | bytes 2097152 | tf_op jit(solution)/shard_map/all_to_all | solution.py:86
  65.4 6.9 %all-to-all-start.4 = ((bf16[4,64,2]{1,2,0:T(2,128)(2,1)}), bf16[4,64,2]{1,2,0:T(2,128)(2,1)S(1)}, u32[]{:S(2)}, u32[]{:S(2)}) async-start(bf16[4,64,2]{1,2,0:T(2,128)(2,1)} %copy.51), calls=%async_computation.4 | async-start | bytes 4096 | tf_op jit(solution)/shard_map/all_to_all | solution.py:127
  77.3 0.6 copy-start.8
  82.8 6.9 %all-to-all-start = ((bf16[4,64,2]{1,2,0:T(2,128)(2,1)}), bf16[4,64,2]{1,2,0:T(2,128)(2,1)S(1)}, u32[]{:S(2)}, u32[]{:S(2)}) async-start(bf16[4,64,2]{1,2,0:T(2,128)(2,1)} %copy.49), calls=%async_computation | async-start | bytes 4096 | tf_op jit(solution)/shard_map/all_to_all | solution.py:93
  86.0 265.2 %all-reduce.2.cloned.1.call-start = ((), (), s32[]{:S(2)}) async-start(), calls=%async_computation.7 | async-start | bytes 2097152 | tf_op jit(solution)/shard_map/psum | solution.py:156
  89.2 276.1 %reduce-scatter.5.cloned.1.call-start = ((), (), s32[]{:S(2)}) async-start(), calls=%async_computation.9 | async-start | bytes 7077888 | tf_op jit(solution)/shard_map/reduce_scatter | solution.py:163
  95.7 336.9 %reduce-scatter.3.cloned.1.call-start = ((), (), s32[]{:S(2)}) async-start(), calls=%async_computation.8 | async-start | bytes 14155776 | tf_op jit(solution)/shard_map/reduce_scatter | solution.py:160
  117.8 236.0 %copy-start.10 = (s32[1024]{0:T(1024)S(1)}, s32[1024]{0:T(1024)}, u32[]{:S(2)}) copy-start(s32[1024]{0:T(1024)} %copy-done.9) | copy-start | bytes 12292
  117.8 236.0 %all-to-all-start.3 = ((bf16[4,64,2048]{2,1,0:T(8,128)(2,1)}), bf16[4,64,2048]{2,1,0:T(8,128)(2,1)S(1)}, u32[]{:S(2)}, u32[]{:S(2)}) async-start(bf16[4,64,2048]{2,1,0:T(8,128)(2,1)} %bitcast.9), calls=%async_computation.3 | async-start | bytes 2097152 | tf_op jit(solution)/shard_map/all_to_all | solution.py:120
  356.3 2.3 copy-start.6
  356.3 76.3 %copy-start.1 = (bf16[128,2048]{1,0:T(8,128)(2,1)S(1)}, bf16[128,2048]{1,0:T(8,128)(2,1)}, u32[]{:S(2)}) copy-start(bf16[128,2048]{1,0:T(8,128)(2,1)} %param.7) | copy-start | bytes 1572868
  358.6 5.6 %copy-start.4 = (bf16[2048,128]{1,0:T(8,128)(2,1)S(1)}, bf16[2048,128]{1,0:T(8,128)(2,1)}, u32[]{:S(2)}) copy-start(bf16[2048,128]{1,0:T(8,128)(2,1)} %param.10) | copy-start | bytes 1572868
Sparse Core Ops, SparseCore 0:
  92.6 258.5 all-reduce.1
Sparse Core Ops, SparseCore 1:
  95.8 123.6 reduce-scatter.4
  223.5 209.1 reduce-scatter.2
where the time goes:
time: 441 us; the launch traced here: 440 us
  waiting for transfers between devices  316 us (72%)
  matrix products  43.3 us (10%)
  local copies, waits for them, and re-layouts  26.9 us (6%)
  other arithmetic  19.7 us (4%)
  starting transfers between devices  18.5 us (4%)
  between operations  15.8 us (4%)
    psum x1, waiting for transfers between devices, per_device(): router_grad = lax.psum(router_part, ('dp', 'expert'))  230 us
    reduce_scatter x1, waiting for transfers between devices, per_device(): lax.psum_scatter(part_gateup[None], 'dp', scatter_dimension=1, tiled=True)  67.3 us
    all_to_all x1, waiting for transfers between devices, per_device(): lax.all_to_all(send_in.reshape(flight, capacity, width), 'expert', split_...  13.1 us
    dot_general x1, matrix products, expert_rows(): pre_act = jnp.dot(rows_in, w_gateup, preferred_element_type=jnp.float32)  9.69 us
    dot_general x1, matrix products, expert_rows(): lax.dot_general(pre_grad, w_gateup, (((1,), (1,)), ((), ())), preferred_e...  9.05 us
  transfers between devices with their start and end apart: 8, of which 6 were waited for; matrix products, arithmetic and copies ran while one was open for 13% of the time, Pallas kernels for 0%

commit v1 on v0

--- a/solution.py
+++ b/solution.py
@@ -153,7 +153,7 @@
     router_part = lax.dot_general(
         tokens, logit_grad, (((0,), (0,)), ((), ())), preferred_element_type=jnp.float32
     )
-    router_grad = lax.psum(router_part, ("dp", "expert"))
+    router_grad = lax.psum(lax.psum(router_part, "dp"), "expert")
     part_gateup = acc_gateup.astype(jnp.bfloat16)
     part_down = acc_down.astype(jnp.bfloat16)
     gate_up_grad, down_grad = (

time: 441 us -> 544 us (1.23)
  waiting for transfers between devices: 316 us -> 403 us
  blocking collectives: 0 us -> 29 us
  starting transfers between devices: 18.5 us -> 11.5 us
    psum x1 -> x2, waiting for transfers between devices: 230 us -> 69.5 us  [per_device(): router_grad = lax.psum(lax.psum(router_part, 'dp'), 'expert')]
    reduce_scatter x1, waiting for transfers between devices: 67.3 us -> 211 us  [per_device(): lax.psum_scatter(part_gateup[None], 'dp', scatter_dimension=1, tiled=True)]
    reduce_scatter x1, waiting for transfers between devices: 0.01 us -> 105 us  [per_device(): lax.psum_scatter(part_down[None], 'dp', scatter_dimension=1, tiled=True)]
    all_to_all x0 -> x2, blocking collectives: none -> 29 us  [the longest x1 22.9 us: per_device(): lax.all_to_all(back_rows.reshape(sources, capacity, width), 'expert', spl...]
    all_to_all x2 -> x0, starting transfers between devices: 7.09 us -> none  [the longest x1 3.87 us: per_device(): lax.all_to_all(back_rows.reshape(sources, capacity, width), 'expert', spl...]
  transfers between devices with their start and end apart: 8 -> 7, of which waited for: 6 -> 6; matrix products, arithmetic and copies ran while one was open for 13% -> 11% of each run, Pallas kernels for 0% -> 0%
where the time goes in v1:
time: 544 us
  waiting for transfers between devices  403 us (74%)
  matrix products  42.6 us (8%)
  blocking collectives  29 us (5%)
  local copies, waits for them, and re-layouts  25.7 us (5%)
  other arithmetic  17.3 us (3%)
  between operations  14.1 us (3%)
  starting transfers between devices  11.5 us (2%)
    reduce_scatter x1, waiting for transfers between devices, per_device(): lax.psum_scatter(part_gateup[None], 'dp', scatter_dimension=1, tiled=True)  211 us
    reduce_scatter x1, waiting for transfers between devices, per_device(): lax.psum_scatter(part_down[None], 'dp', scatter_dimension=1, tiled=True)  105 us
    psum x2, waiting for transfers between devices, per_device(): router_grad = lax.psum(lax.psum(router_part, 'dp'), 'expert')  69.5 us
    all_to_all x1, blocking collectives, per_device(): lax.all_to_all(back_rows.reshape(sources, capacity, width), 'expert', spl...  22.9 us
    all_to_all x1, waiting for transfers between devices, per_device(): lax.all_to_all(send_in.reshape(flight, capacity, width), 'expert', split_...  13.1 us
  transfers between devices with their start and end apart: 7, of which 6 were waited for; matrix products, arithmetic and copies ran while one was open for 11% of the time, Pallas kernels for 0%

profile of v1, /device:TPU:0, one launch (start us, length us, event | category | flops | bytes accessed | tf_op | source)
XLA Modules:
  0.0 543.6 jit_solution(13013839891197101313)
XLA Ops:
  7.2 0.7 broadcast_compare_fusion
  7.9 0.7 broadcast_multiply_fusion
  8.6 0.8 copy.45
  9.8 0.6 copy-done.5
  10.7 1.2 reduce-window.6
  12.5 2.4 scatter_custom_fusion.1
  14.9 2.4 scatter_custom_fusion
  17.5 0.6 pad_clamp_fusion.1
  18.1 1.4 gather_fusion.2
  19.5 1.4 gather_fusion.1
  20.8 1.5 broadcast_select_fusion
  22.4 4.4 all-to-all-start.2
  26.8 0.4 exponential_reduce_fusion
  27.5 0.5 multiply_multiply_fusion
  28.1 13.1 %all-to-all-done.2 = bf16[4,64,2048]{2,1,0:T(8,128)(2,1)S(1)} async-done(((bf16[4,64,2048]{2,1,0:T(8,128)(2,1)}), bf16[4,64,2048]{2,1,0:T(8,128)(2,1)S(1)}, u32[]{:S(2)}, u32[]{:S(2)}) %all-to-all-start.2) | async-done | bytes 1048608 | tf_op jit(solution)/shard_map/all_to_all | solution.py:79
  41.2 3.5 all-to-all-start.1
  44.7 9.7 %fusion.2 = f32[256,3072]{1,0:T(8,128)} fusion(bf16[256,2048]{1,0:T(8,128)(2,1)S(1)} %bitcast.81, bf16[1,2048,3072]{2,1,0:T(8,128)(2,1)} %param.12), kind=kOutput, calls=%fused_computation.9 | convolution fusion | flops 3221225472 | bytes 16777216 | tf_op jit(solution)/shard_map/dot_general | solution.py:9
  54.4 2.3 multiply_convert_fusion.1
  56.7 2.4 all-to-all-done.1
  59.1 4.8 fusion.24
  64.0 0.6 copy.51
  64.6 3.2 all-to-all-start.4
  68.0 0.5 exponential_reduce_fusion.1
  68.6 2.9 all-to-all-done.4
  71.6 3.5 gather_fusion.4
  75.3 0.7 multiply_reduce_fusion
  76.2 0.7 copy.54
  76.9 0.9 add_convert_fusion
  77.8 1.3 convolution_bitcast_fusion
  79.3 2.1 gather_fusion
  81.7 6.1 %all_to_all.25 = bf16[4,64,2]{1,2,0:T(2,128)(2,1)S(1)} all-to-all(bf16[4,64,2]{1,2,0:T(2,128)(2,1)S(1)} %copy.49), channel_id=1, replica_groups=mesh['dp'=8,'expert'=4] {'expert'}, dimensions={0} | all-to-all | bytes 2048 | tf_op jit(solution)/shard_map/all_to_all | solution.py:93
  87.9 0.5 broadcast.186
  88.4 0.7 fusion.38
  89.0 69.5 %all-reduce.3.cloned.1.call-done = f32[2048,128]{0,1:T(8,128)} async-done(((f32[2048,128]{0,1:T(8,128)}), f32[2048,128]{0,1:T(8,128)}) %all-reduce.3.cloned.1.call-update) | async-done | bytes 1048592 | tf_op jit(solution)/shard_map/psum | solution.py:156
  158.6 0.2 fusion.22
  158.8 4.4 fusion.4
  163.4 0.2 multiply_convert_fusion
  163.7 6.2 %multiply_convert_fusion.3 = (bf16[256,1536]{1,0:T(8,128)(2,1)S(1)}, bf16[256,1536]{1,0:T(8,128)(2,1)S(1)}) fusion(f32[256,3072]{1,0:T(8,128)} %fusion.2, bf16[256,2048]{1,0:T(8,128)(2,1)S(1)} %bitcast.85, bf16[1,1536,2048]{2,1,0:T(8,128)(2,1)} %param.13), kind=kOutput, calls=%fused_computation.32 | convolution fusion | flops 1615724544 | bytes 12058624 | tf_op jit(solution)/shard_map/dot_general | solution.py:15
  169.9 6.6 %convert_bitcast_fusion = bf16[1,2048,3072]{2,1,0:T(8,128)(2,1)} fusion(bf16[256,2048]{1,0:T(8,128)(2,1)S(1)} %bitcast.82, bf16[256,1536]{1,0:T(8,128)(2,1)S(1)} %get-tuple-element.31, bf16[256,1536]{1,0:T(8,128)(2,1)S(1)} %get-tuple-element.30), kind=kOutput, calls=%fused_computation.11 | convolution fusion | flops 3230662656 | bytes 15204352 | tf_op jit(solution)/shard_map/dot_general | solution.py:25
  176.5 8.1 %fusion.18 = bf16[256,2048]{1,0:T(8,128)(2,1)S(1)} fusion(bf16[1,2048,3072]{2,1,0:T(8,128)(2,1)} %param.12, bf16[256,1536]{1,0:T(8,128)(2,1)S(1)} %get-tuple-element.31, bf16[256,1536]{1,0:T(8,128)(2,1)S(1)} %get-tuple-element.30), kind=kOutput, calls=%fused_computation.22 | convolution fusion | flops 3224895488 | bytes 15204352 | tf_op jit(solution)/shard_map/dot_general | solution.py:28
  184.7 22.9 %all_to_all.26 = bf16[4,64,2048]{2,1,0:T(8,128)(2,1)S(1)} all-to-all(bf16[4,64,2048]{2,1,0:T(8,128)(2,1)S(1)} %bitcast.86), channel_id=1, replica_groups=mesh['dp'=8,'expert'=4] {'expert'}, dimensions={0} | all-to-all | bytes 2097152 | tf_op jit(solution)/shard_map/all_to_all | solution.py:120
  207.6 2.5 gather_fusion.3
  210.1 2.2 gather.29
  212.3 5.6 %convert_reduce_fusion = f32[128,2048]{1,0:T(8,128)S(1)} fusion(bf16[128,4,2048]{2,1,0:T(4,128)(2,1)} %gather.29, pred[128,4]{1,0:T(8,128)(4,1)S(1)} %copy-done.6), kind=kLoop, calls=%fused_computation.18 | loop fusion | flops 2883584 | bytes 3146240 | tf_op jit(solution)/shard_map/reduce_sum | solution.py:148
  217.9 1.1 fusion.21
  219.1 2.5 copy.55
  221.6 104.8 %reduce-scatter.5.cloned.1.call-done = bf16[1,192,2048]{2,1,0:T(8,128)(2,1)} async-done(((bf16[1,1536,2048]{2,1,0:T(8,128)(2,1)}), bf16[1,192,2048]{2,1,0:T(8,128)(2,1)}) %reduce-scatter.5.cloned.1.call-update) | async-done | bytes 786448 | tf_op jit(solution)/shard_map/reduce_scatter | solution.py:163
  326.4 210.7 %reduce-scatter.3.cloned.1.call-done = bf16[1,256,3072]{2,1,0:T(8,128)(2,1)} async-done(((bf16[1,2048,3072]{2,1,0:T(8,128)(2,1)}), bf16[1,256,3072]{2,1,0:T(8,128)(2,1)}) %reduce-scatter.3.cloned.1.call-update) | async-done | bytes 1572880 | tf_op jit(solution)/shard_map/reduce_scatter | solution.py:160
  (74 shorter events, 3.3 us)
Async XLA Ops:
  7.2 10.9 %copy-start = (bf16[128,2048]{1,0:T(8,128)(2,1)S(1)}, bf16[128,2048]{1,0:T(8,128)(2,1)}, u32[]{:S(2)}) copy-start(bf16[128,2048]{1,0:T(8,128)(2,1)} %param.7) | copy-start | bytes 1572868
  9.8 0.6 copy-start.5
  17.4 0.7 copy-start.10
  18.1 1.4 copy-start.2
  22.4 4.4 copy-start.3
  22.4 4.9 copy-start.7
  22.4 5.1 copy-start.12
  22.4 18.8 %all-to-all-start.2 = ((bf16[4,64,2048]{2,1,0:T(8,128)(2,1)}), bf16[4,64,2048]{2,1,0:T(8,128)(2,1)S(1)}, u32[]{:S(2)}, u32[]{:S(2)}) async-start(bf16[4,64,2048]{2,1,0:T(8,128)(2,1)} %get-tuple-element.38), calls=%async_computation.2 | async-start | bytes 2097152 | tf_op jit(solution)/shard_map/all_to_all | solution.py:79
  27.2 44.3 %copy-start.8 = (s32[1024]{0:T(1024)}, s32[1024]{0:T(1024)S(1)}, u32[]{:S(2)}) copy-start(s32[1024]{0:T(1024)S(1)} %pad_clamp_fusion) | copy-start | bytes 12292
  41.2 17.9 %all-to-all-start.1 = ((bf16[4,64,2048]{2,1,0:T(8,128)(2,1)}), bf16[4,64,2048]{2,1,0:T(8,128)(2,1)S(1)}, u32[]{:S(2)}, u32[]{:S(2)}) async-start(bf16[4,64,2048]{2,1,0:T(8,128)(2,1)} %get-tuple-element.39), calls=%async_computation.1 | async-start | bytes 2097152 | tf_op jit(solution)/shard_map/all_to_all | solution.py:86
  64.6 6.9 %all-to-all-start.4 = ((bf16[4,64,2]{1,2,0:T(2,128)(2,1)}), bf16[4,64,2]{1,2,0:T(2,128)(2,1)S(1)}, u32[]{:S(2)}, u32[]{:S(2)}) async-start(bf16[4,64,2]{1,2,0:T(2,128)(2,1)} %copy.51), calls=%async_computation.4 | async-start | bytes 4096 | tf_op jit(solution)/shard_map/all_to_all | solution.py:127
  67.8 90.7 %all-reduce.3.cloned.1.call-start = ((), (), s32[]{:S(2)}) async-start(), calls=%async_computation.7 | async-start | bytes 2097152 | tf_op jit(solution)/shard_map/psum | solution.py:156
  76.0 5.5 %copy-start.11 = (pred[256]{0:T(512)(128)(4,1)S(1)}, pred[256]{0:T(512)(128)(4,1)}, u32[]{:S(2)}) copy-start(pred[256]{0:T(512)(128)(4,1)} %copy-done.10) | copy-start | bytes 772
  79.1 140.0 %all-reduce.5.cloned.1.call-start = ((), (), s32[]{:S(2)}) async-start(), calls=%async_computation.8 | async-start | bytes 2097152 | tf_op jit(solution)/shard_map/psum | solution.py:156
  158.5 167.8 %reduce-scatter.5.cloned.1.call-start = ((), (), s32[]{:S(2)}) async-start(), calls=%async_computation.10 | async-start | bytes 7077888 | tf_op jit(solution)/shard_map/reduce_scatter | solution.py:163
  163.3 373.8 %reduce-scatter.3.cloned.1.call-start = ((), (), s32[]{:S(2)}) async-start(), calls=%async_computation.9 | async-start | bytes 14155776 | tf_op jit(solution)/shard_map/reduce_scatter | solution.py:160
  184.7 22.9 %copy-start.9 = (s32[1024]{0:T(1024)S(1)}, s32[1024]{0:T(1024)}, u32[]{:S(2)}) copy-start(s32[1024]{0:T(1024)} %copy-done.8) | copy-start | bytes 12292
  210.1 2.3 copy-start.6
  212.3 5.6 %copy-start.4 = (bf16[2048,128]{1,0:T(8,128)(2,1)S(1)}, bf16[2048,128]{1,0:T(8,128)(2,1)}, u32[]{:S(2)}) copy-start(bf16[2048,128]{1,0:T(8,128)(2,1)} %param.10) | copy-start | bytes 1572868
  212.3 324.8 %copy-start.1 = (bf16[128,2048]{1,0:T(8,128)(2,1)S(1)}, bf16[128,2048]{1,0:T(8,128)(2,1)}, u32[]{:S(2)}) copy-start(bf16[128,2048]{1,0:T(8,128)(2,1)} %param.7) | copy-start | bytes 1572868
Sparse Core Ops, SparseCore 0:
  79.2 79.2 all-reduce.2
  160.9 42.0 all-reduce.4
  207.1 119.2 reduce-scatter.4
  330.4 206.6 reduce-scatter.2
